TPU v7x, 32 devices: a 4x4x1 block of a 4x4x8 slice. The times are simulated.
32 devices in a mesh: dp: 1 (over z), sp: 4 (over y), beam: 8 (over x, core).
Axes of the slice: x: 4, y: 4, z: 1, core: 2. Of those that a mesh axis runs over, the one named last changes fastest.
The devices are a block of a 4x4x8 slice.
Arguments:
- tok_emb: bfloat16 [48, 512], P(('dp', 'beam'))
- parent: int32 [2, 24], P('dp')
- position: int32 [1], replicated
- beam_score: float32 [48], P(('dp', 'beam'))
- k_cache: bfloat16 [2, 48, 1024, 8, 64], P(None, ('dp', 'beam'), 'sp')
- v_cache: bfloat16 [2, 48, 1024, 8, 64], P(None, ('dp', 'beam'), 'sp')
- w_query: bfloat16 [2, 512, 512], replicated
- w_key: bfloat16 [2, 512, 512], replicated
- w_value: bfloat16 [2, 512, 512], replicated
- w_out: bfloat16 [2, 512, 512], replicated
- w_gate: bfloat16 [2, 512, 2048], replicated
- w_up: bfloat16 [2, 512, 2048], replicated
- w_down: bfloat16 [2, 2048, 512], replicated
- g_attn: bfloat16 [2, 512], replicated
- g_mlp: bfloat16 [2, 512], replicated
- g_final: bfloat16 [512], replicated
- w_vocab: bfloat16 [512, 32128], replicated
Outputs:
- output 1: bfloat16 [2, 48, 1024, 8, 64], P(None, ('dp', 'beam'), 'sp')
- output 2: bfloat16 [2, 48, 1024, 8, 64], P(None, ('dp', 'beam'), 'sp')
- output 3: float32 [48, 32128], P(('dp', 'beam'))
All inputs are finite; a program needn't handle non-finite values.
Results may differ from a plain program's by a relative error of at most 0.00207768.
Values are sent between devices in bfloat16 or wider.
A program may use at most 768 MiB of HBM per device.

v0:
```python
import jax
import jax.numpy as jnp
from jax import lax
from jax.sharding import PartitionSpec as P, NamedSharding

ROPE_BASE = 10000.0
NORM_EPS = 1e-6


def rms_norm(x_in, g_vec):
    mean_sq = jnp.mean(x_in * x_in, axis=-1, keepdims=True)
    return (x_in * lax.rsqrt(mean_sq + NORM_EPS) * g_vec.astype(jnp.float32)).astype(jnp.bfloat16)


def rope_at(x_in, cur_pos):
    half_dim = x_in.shape[-1] // 2
    inv_freq = ROPE_BASE ** (-2.0 * jnp.arange(half_dim, dtype=jnp.float32) / x_in.shape[-1])
    angles = cur_pos.astype(jnp.float32) * inv_freq
    cos_t = jnp.cos(angles)
    sin_t = jnp.sin(angles)
    x_f = x_in.astype(jnp.float32)
    x_lo = x_f[..., :half_dim]
    x_hi = x_f[..., half_dim:]
    rotated = jnp.concatenate([x_lo * cos_t - x_hi * sin_t, x_hi * cos_t + x_lo * sin_t], axis=-1)
    return rotated.astype(jnp.bfloat16)


def solution(mesh):
    beam_spec = P(('dp', 'beam'))
    row_spec = P(('dp', 'beam'), None)
    cache_spec = P(None, ('dp', 'beam'), 'sp', None, None)
    full_rep = P()

    def local_step(tok_emb, parent, position, beam_score, k_cache, v_cache, w_query, w_key, w_value, w_out, w_gate, w_up, w_down, g_attn, g_mlp, g_final, w_vocab):
        group_devs = mesh.shape['beam']
        n_layers, local_beams, local_slots, kv_heads, head_dim = k_cache.shape
        beam_width = parent.shape[1]
        span_devs = beam_width // local_beams
        n_heads = w_query.shape[-1] // head_dim
        q_groups = n_heads // kv_heads
        att_scale = head_dim ** -0.5
        my_idx = lax.axis_index('beam')
        seq_idx = lax.axis_index('sp')
        cur_pos = position[0]
        my_parents = lax.dynamic_slice(parent.reshape(-1), (my_idx * local_beams,), (local_beams,))
        src_devs = my_parents // local_beams
        src_rows = my_parents % local_beams
        col_ids = jnp.arange(local_beams, dtype=jnp.int32)
        block_start = (my_idx // span_devs) * span_devs
        my_place = my_idx - block_start

        def pick_rows(cache_blk, from_dev):
            one_hot = ((src_devs == from_dev)[:, None] & (src_rows[:, None] == col_ids[None, :])).astype(jnp.bfloat16)
            flat_rows = cache_blk.reshape(n_layers, local_beams, -1)
            picked = jnp.einsum('rc,lcx->lrx', one_hot, flat_rows, preferred_element_type=jnp.float32)
            return picked.astype(jnp.bfloat16)

        k_flat = pick_rows(k_cache, my_idx)
        v_flat = pick_rows(v_cache, my_idx)
        for shift_by in range(1, span_devs):
            perm_pairs = [(sender, (sender // span_devs) * span_devs + (sender % span_devs + shift_by) % span_devs) for sender in range(group_devs)]
            k_recv, v_recv = lax.ppermute((k_cache, v_cache), 'beam', perm_pairs)
            from_dev = block_start + (my_place - shift_by) % span_devs
            k_flat = k_flat + pick_rows(k_recv, from_dev)
            v_flat = v_flat + pick_rows(v_recv, from_dev)
        k_new = k_flat.reshape(k_cache.shape)
        v_new = v_flat.reshape(v_cache.shape)
        all_scores = lax.all_gather(beam_score, 'beam', tiled=True)
        parent_score = jnp.take(all_scores, my_parents)
        slot_base = seq_idx * local_slots
        slot_valid = slot_base + jnp.arange(local_slots) <= cur_pos
        owns_pos = (cur_pos >= slot_base) & (cur_pos < slot_base + local_slots)
        slot_at = jnp.clip(cur_pos - slot_base, 0, local_slots - 1)
        row_shape = (1, local_beams, 1, kv_heads, head_dim)
        residual = tok_emb.astype(jnp.float32)
        for layer_idx in range(n_layers):
            hidden = rms_norm(residual, g_attn[layer_idx])
            queries = rope_at(jnp.dot(hidden, w_query[layer_idx], preferred_element_type=jnp.float32).astype(jnp.bfloat16).reshape(local_beams, kv_heads, q_groups, head_dim), cur_pos)
            key_new = rope_at(jnp.dot(hidden, w_key[layer_idx], preferred_element_type=jnp.float32).astype(jnp.bfloat16).reshape(row_shape), cur_pos)
            val_new = jnp.dot(hidden, w_value[layer_idx], preferred_element_type=jnp.float32).astype(jnp.bfloat16).reshape(row_shape)
            start_at = (layer_idx, 0, slot_at, 0, 0)
            old_key = lax.dynamic_slice(k_new, start_at, row_shape)
            old_val = lax.dynamic_slice(v_new, start_at, row_shape)
            k_new = lax.dynamic_update_slice(k_new, jnp.where(owns_pos, key_new, old_key), start_at)
            v_new = lax.dynamic_update_slice(v_new, jnp.where(owns_pos, val_new, old_val), start_at)
            scores = jnp.einsum('bkgd,bskd->bkgs', queries, k_new[layer_idx], preferred_element_type=jnp.float32) * att_scale
            scores = jnp.where(slot_valid, scores, -jnp.inf)
            row_max = lax.pmax(jnp.max(scores, axis=-1, keepdims=True), 'sp')
            exp_scores = jnp.exp(scores - row_max)
            part_sum = jnp.sum(exp_scores, axis=-1)
            part_mix = jnp.einsum('bkgs,bskd->bkgd', exp_scores.astype(jnp.bfloat16), v_new[layer_idx], preferred_element_type=jnp.float32)
            mix_sum, exp_total = lax.psum((part_mix, part_sum), 'sp')
            attn_out = (mix_sum / exp_total[..., None]).astype(jnp.bfloat16).reshape(local_beams, n_heads * head_dim)
            residual = residual + jnp.dot(attn_out, w_out[layer_idx], preferred_element_type=jnp.float32).astype(jnp.bfloat16).astype(jnp.float32)
            hidden = rms_norm(residual, g_mlp[layer_idx])
            gate_act = jnp.dot(hidden, w_gate[layer_idx], preferred_element_type=jnp.float32).astype(jnp.bfloat16)
            up_act = jnp.dot(hidden, w_up[layer_idx], preferred_element_type=jnp.float32).astype(jnp.bfloat16)
            swi_out = (jax.nn.silu(gate_act.astype(jnp.float32)) * up_act.astype(jnp.float32)).astype(jnp.bfloat16)
            residual = residual + jnp.dot(swi_out, w_down[layer_idx], preferred_element_type=jnp.float32).astype(jnp.bfloat16).astype(jnp.float32)
        hidden = rms_norm(residual, g_final)
        logits = jnp.dot(hidden, w_vocab, preferred_element_type=jnp.float32)
        candidates = parent_score[:, None] + jax.nn.log_softmax(logits, axis=-1)
        return k_new, v_new, candidates

    in_specs = (row_spec, P('dp', None), full_rep, beam_spec, cache_spec, cache_spec) + (full_rep,) * 11
    return jax.shard_map(local_step, mesh=mesh, in_specs=in_specs, out_specs=(cache_spec, cache_spec, row_spec), check_vma=False)
```

profile of v0, /device:TPU:96, one launch (start us, length us, event | category | flops | bytes accessed | tf_op | source)
XLA Modules:
  0.0 548.1 jit_solution(3711356420055433154)
XLA Ops:
  12.1 234.1 %all-reduce = f32[48]{0:T(128)S(1)} all-reduce(f32[48]{0:T(128)S(1)} %dynamic-update-slice), channel_id=1, replica_groups=mesh['dp'=1,'sp'=4,'beam'=8] {'beam'}, use_global_device_ids=true, to_apply=%add | all-reduce | flops 48 | bytes 384
  250.5 7.1 %copy.100 = bf16[2,6,256,8,64]{4,3,2,1,0:T(8,128)(2,1)} copy(bf16[2,6,256,8,64]{2,4,3,1,0:T(8,128)(2,1)} %param.21) | data formatting | bytes 6291456 | tf_op jit(solution)/shard_map/reshape | solution.py:54
  257.6 7.1 %copy.104 = bf16[2,6,256,8,64]{4,3,2,1,0:T(8,128)(2,1)} copy(bf16[2,6,256,8,64]{2,4,3,1,0:T(8,128)(2,1)} %param.22) | data formatting | bytes 6291456 | tf_op jit(solution)/shard_map/reshape | solution.py:54
  264.7 8.4 %reshape.368 = bf16[2,6,131072]{2,1,0:T(8,128)(2,1)} reshape(bf16[2,6,256,8,64]{4,3,2,1,0:T(8,128)(2,1)} %copy.100) | data formatting | bytes 6291456 | tf_op jit(solution)/shard_map/reshape | solution.py:54
  273.2 8.4 %reshape.372 = bf16[2,6,131072]{2,1,0:T(8,128)(2,1)} reshape(bf16[2,6,256,8,64]{4,3,2,1,0:T(8,128)(2,1)} %copy.104) | data formatting | bytes 6291456 | tf_op jit(solution)/shard_map/reshape | solution.py:54
  291.3 7.1 %copy.103 = bf16[2,6,256,8,64]{4,3,2,1,0:T(8,128)(2,1)} copy(bf16[2,6,256,8,64]{2,4,3,1,0:T(8,128)(2,1)} %collective-permute-done.2) | data formatting | bytes 6291456 | tf_op jit(solution)/shard_map/reshape | solution.py:54
  298.4 8.4 %reshape.371 = bf16[2,6,131072]{2,1,0:T(8,128)(2,1)} reshape(bf16[2,6,256,8,64]{4,3,2,1,0:T(8,128)(2,1)} %copy.103) | data formatting | bytes 6291456 | tf_op jit(solution)/shard_map/reshape | solution.py:54
  306.8 7.1 %copy.102 = bf16[2,6,256,8,64]{4,3,2,1,0:T(8,128)(2,1)} copy(bf16[2,6,256,8,64]{2,4,3,1,0:T(8,128)(2,1)} %collective-permute-done.1) | data formatting | bytes 6291456 | tf_op jit(solution)/shard_map/reshape | solution.py:54
  313.8 8.4 %reshape.370 = bf16[2,6,131072]{2,1,0:T(8,128)(2,1)} reshape(bf16[2,6,256,8,64]{4,3,2,1,0:T(8,128)(2,1)} %copy.102) | data formatting | bytes 6291456 | tf_op jit(solution)/shard_map/reshape | solution.py:54
  327.5 8.5 %reshape.369 = bf16[2,6,131072]{2,1,0:T(8,128)(2,1)} reshape(bf16[2,6,256,8,64]{4,3,2,1,0:T(8,128)(2,1)} %copy.101) | data formatting | bytes 6291456 | tf_op jit(solution)/shard_map/reshape | solution.py:54
  360.5 7.1 %copy.107 = bf16[2,6,256,8,64]{4,3,2,1,0:T(8,128)(2,1)} copy(bf16[2,6,256,8,64]{2,4,3,1,0:T(8,128)(2,1)} %collective-permute-done.5) | data formatting | bytes 6291456 | tf_op jit(solution)/shard_map/reshape | solution.py:54
  367.6 8.4 %reshape.375 = bf16[2,6,131072]{2,1,0:T(8,128)(2,1)} reshape(bf16[2,6,256,8,64]{4,3,2,1,0:T(8,128)(2,1)} %copy.107) | data formatting | bytes 6291456 | tf_op jit(solution)/shard_map/reshape | solution.py:54
  376.0 7.1 %copy.106 = bf16[2,6,256,8,64]{4,3,2,1,0:T(8,128)(2,1)} copy(bf16[2,6,256,8,64]{2,4,3,1,0:T(8,128)(2,1)} %collective-permute-done.4) | data formatting | bytes 6291456 | tf_op jit(solution)/shard_map/reshape | solution.py:54
  383.1 8.6 %reshape.374 = bf16[2,6,131072]{2,1,0:T(8,128)(2,1)} reshape(bf16[2,6,256,8,64]{4,3,2,1,0:T(8,128)(2,1)} %copy.106) | data formatting | bytes 6291456 | tf_op jit(solution)/shard_map/reshape | solution.py:54
  400.5 7.1 %copy.105 = bf16[2,6,256,8,64]{4,3,2,1,0:T(8,128)(2,1)} copy(bf16[2,6,256,8,64]{2,4,3,1,0:T(8,128)(2,1)} %collective-permute-done.3) | data formatting | bytes 6291456 | tf_op jit(solution)/shard_map/reshape | solution.py:54
  407.6 8.6 %reshape.373 = bf16[2,6,131072]{2,1,0:T(8,128)(2,1)} reshape(bf16[2,6,256,8,64]{4,3,2,1,0:T(8,128)(2,1)} %copy.105) | data formatting | bytes 6291456 | tf_op jit(solution)/shard_map/reshape | solution.py:54
  416.2 7.2 %fusion.7 = bf16[2,6,131072]{2,1,0:T(8,128)(2,1)S(1)} fusion(bf16[6,2,131072]{2,0,1:T(8,128)(2,1)} %convolution_convert_fusion, bf16[6,2,131072]{2,0,1:T(8,128)(2,1)} %convolution_convert_fusion.1, bf16[6,2,131072]{2,0,1:T(8,128)(2,1)} %convolution_convert_fusion.3, bf16[2,6,131072]{2,1,0:T(8,128)(2,1)} %reshape.373, s32[6]{0:T(128)S(1)} %get-tuple-element.32, ...), kind=kOutput, calls=%fused_computation.16 | convolution fusion | flops 25165896 | bytes 15728670 | tf_op jit(solution)/shard_map/rc,lcx->lrx/dot_general | solution.py:55
  440.3 12.4 %pmax.14 = f32[6,8]{1,0:T(8,128)S(1)} all-reduce(f32[6,8]{1,0:T(8,128)S(1)} %fusion.116), channel_id=1, replica_groups=mesh['dp'=1,'sp'=4,'beam'=8] {'sp'}, use_global_device_ids=true, to_apply=%region_2.3 | all-reduce | flops 48 | bytes 384 | tf_op jit(solution)/shard_map/pmax | solution.py:88
  453.3 14.6 %all-reduce.2 = (f32[6,8,1,64]{3,1,0,2:T(8,128)S(1)}, f32[6,8]{1,0:T(8,128)S(1)}) all-reduce(f32[6,8,1,64]{3,1,0,2:T(8,128)S(1)} %bitcast.226, f32[6,8]{1,0:T(8,128)S(1)} %get-tuple-element.17), channel_id=1, replica_groups=mesh['dp'=1,'sp'=4,'beam'=8] {'sp'}, use_global_device_ids=true, to_apply=%region_3.4 | all-reduce | flops 3120 | bytes 24960 | tf_op jit(solution)/shard_map/psum | solution.py:92
  476.4 7.1 %copy.87 = bf16[2,6,256,8,64]{2,4,3,1,0:T(8,128)(2,1)} copy(bf16[2,6,256,8,64]{4,3,2,0,1:T(8,128)(2,1)} %fusion.131) | data formatting | bytes 6291456
  488.8 7.1 %copy.86 = bf16[2,6,256,8,64]{2,4,3,1,0:T(8,128)(2,1)} copy(bf16[2,6,256,8,64]{4,3,2,0,1:T(8,128)(2,1)} %fusion.130) | data formatting | bytes 6291456
  499.5 9.6 %pmax.15 = f32[6,8]{1,0:T(8,128)S(1)} all-reduce(f32[6,8]{1,0:T(8,128)S(1)} %fusion.117), channel_id=1, replica_groups=mesh['dp'=1,'sp'=4,'beam'=8] {'sp'}, use_global_device_ids=true, to_apply=%region_9.10 | all-reduce | flops 48 | bytes 384 | tf_op jit(solution)/shard_map/pmax | solution.py:88
  511.7 14.9 %all-reduce.1 = (f32[6,8,1,64]{3,1,0,2:T(8,128)S(1)}, f32[6,8]{1,0:T(8,128)S(1)}) all-reduce(f32[6,8,1,64]{3,1,0,2:T(8,128)S(1)} %bitcast.227, f32[6,8]{1,0:T(8,128)S(1)} %get-tuple-element.15), channel_id=1, replica_groups=mesh['dp'=1,'sp'=4,'beam'=8] {'sp'}, use_global_device_ids=true, to_apply=%region_10.11 | all-reduce | flops 3120 | bytes 24960 | tf_op jit(solution)/shard_map/psum | solution.py:92
  533.2 12.8 %fusion.191 = (f32[6]{0:T(128)S(1)}, f32[6,32128]{1,0:T(8,128)S(1)}) fusion(bf16[512,32128]{1,0:T(8,128)(2,1)} %param.33, f32[6,512]{1,0:T(8,128)S(1)} %get-tuple-element.43, f32[512]{0:T(512)S(1)} %convert_element_type.293, f32[6]{0:T(128)S(1)} %add_rsqrt_fusion), kind=kOutput, calls=%fused_computation.222 | convolution fusion | flops 197596416 | bytes 33684528 | tf_op jit(solution)/shard_map/dot_general | solution.py:101
  (113 shorter events, 108.5 us)
Async XLA Ops:
  0.6 286.9 %collective-permute-start.2 = (bf16[2,6,256,8,64]{2,4,3,1,0:T(8,128)(2,1)}, bf16[2,6,256,8,64]{2,4,3,1,0:T(8,128)(2,1)}, u32[]{:S(2)}, u32[]{:S(2)}) collective-permute-start(bf16[2,6,256,8,64]{2,4,3,1,0:T(8,128)(2,1)} %param.21), channel_id=1, source_target_pairs={{0,3},{1,0},{2,1},{3,2},{4,7},{5,4},{6,5},{7,6},{8,11},{9,8},{10,9... | collective-permute-start | bytes 9437192 | tf_op jit(solution)/shard_map/ppermute | solution.py:62
  1.3 305.5 %collective-permute-start.1 = (bf16[2,6,256,8,64]{2,4,3,1,0:T(8,128)(2,1)}, bf16[2,6,256,8,64]{2,4,3,1,0:T(8,128)(2,1)}, u32[]{:S(2)}, u32[]{:S(2)}) collective-permute-start(bf16[2,6,256,8,64]{2,4,3,1,0:T(8,128)(2,1)} %param.21), channel_id=1, source_target_pairs={{0,2},{1,3},{2,0},{3,1},{4,6},{5,7},{6,4},{7,5},{8,10},{9,11},{10,... | collective-permute-start | bytes 9437192 | tf_op jit(solution)/shard_map/ppermute | solution.py:62
  1.9 320.4 %collective-permute-start = (bf16[2,6,256,8,64]{2,4,3,1,0:T(8,128)(2,1)}, bf16[2,6,256,8,64]{2,4,3,1,0:T(8,128)(2,1)S(1)}, u32[]{:S(2)}, u32[]{:S(2)}) collective-permute-start(bf16[2,6,256,8,64]{2,4,3,1,0:T(8,128)(2,1)} %param.21), channel_id=1, source_target_pairs={{0,1},{1,2},{2,3},{3,0},{4,5},{5,6},{6,7},{7,4},{8,9},{9,10},{10,1... | collective-permute-start | bytes 9437192 | tf_op jit(solution)/shard_map/ppermute | solution.py:62
  2.0 358.5 %collective-permute-start.5 = (bf16[2,6,256,8,64]{2,4,3,1,0:T(8,128)(2,1)}, bf16[2,6,256,8,64]{2,4,3,1,0:T(8,128)(2,1)}, u32[]{:S(2)}, u32[]{:S(2)}) collective-permute-start(bf16[2,6,256,8,64]{2,4,3,1,0:T(8,128)(2,1)} %param.22), channel_id=1, source_target_pairs={{0,3},{1,0},{2,1},{3,2},{4,7},{5,4},{6,5},{7,6},{8,11},{9,8},{10,9... | collective-permute-start | bytes 9437192 | tf_op jit(solution)/shard_map/ppermute | solution.py:62
  3.6 372.4 %collective-permute-start.4 = (bf16[2,6,256,8,64]{2,4,3,1,0:T(8,128)(2,1)}, bf16[2,6,256,8,64]{2,4,3,1,0:T(8,128)(2,1)}, u32[]{:S(2)}, u32[]{:S(2)}) collective-permute-start(bf16[2,6,256,8,64]{2,4,3,1,0:T(8,128)(2,1)} %param.22), channel_id=1, source_target_pairs={{0,2},{1,3},{2,0},{3,1},{4,6},{5,7},{6,4},{7,5},{8,10},{9,11},{10,... | collective-permute-start | bytes 9437192 | tf_op jit(solution)/shard_map/ppermute | solution.py:62
  273.2 8.5 %copy-start.9 = (bf16[512]{0:T(512)(128)(2,1)S(1)}, bf16[512]{0:T(512)(128)(2,1)}, u32[]{:S(2)}) copy-start(bf16[512]{0:T(512)(128)(2,1)} %param.32) | copy-start | bytes 3076
  281.8 6.2 %copy-start = (bf16[2,6,131072]{2,1,0:T(8,128)(2,1)S(1)}, bf16[2,6,131072]{2,1,0:T(8,128)(2,1)}, u32[]{:S(2)}) copy-start(bf16[2,6,131072]{2,1,0:T(8,128)(2,1)} %reshape.372) | copy-start | bytes 9437188
  287.5 113.0 %collective-permute-start.3 = (bf16[2,6,256,8,64]{2,4,3,1,0:T(8,128)(2,1)}, bf16[2,6,256,8,64]{2,4,3,1,0:T(8,128)(2,1)}, u32[]{:S(2)}, u32[]{:S(2)}) collective-permute-start(bf16[2,6,256,8,64]{2,4,3,1,0:T(8,128)(2,1)} %param.22), channel_id=1, source_target_pairs={{0,1},{1,2},{2,3},{3,0},{4,5},{5,6},{6,7},{7,4},{8,9},{9,10},{10,1... | collective-permute-start | bytes 9437192 | tf_op jit(solution)/shard_map/ppermute | solution.py:62
  336.0 5.6 %copy-start.1 = (bf16[2,6,131072]{2,1,0:T(8,128)(2,1)S(1)}, bf16[2,6,131072]{2,1,0:T(8,128)(2,1)}, u32[]{:S(2)}) copy-start(bf16[2,6,131072]{2,1,0:T(8,128)(2,1)} %reshape.370) | copy-start | bytes 9437188
  341.6 3.4 copy-start.3
  341.6 5.0 copy-start.4
  391.7 5.6 %copy-start.2 = (bf16[2,6,131072]{2,1,0:T(8,128)(2,1)S(1)}, bf16[2,6,131072]{2,1,0:T(8,128)(2,1)}, u32[]{:S(2)}) copy-start(bf16[2,6,131072]{2,1,0:T(8,128)(2,1)} %reshape.374) | copy-start | bytes 9437188
  439.3 28.9 %copy-start.8 = (bf16[6,512]{1,0:T(8,128)(2,1)S(1)}, bf16[6,512]{1,0:T(8,128)(2,1)}, u32[]{:S(2)}) copy-start(bf16[6,512]{1,0:T(8,128)(2,1)} %param.17) | copy-start | bytes 18436
  453.3 21.3 %copy-start.5 = (bf16[2,512,512]{2,1,0:T(8,128)(2,1)S(1)}, bf16[2,512,512]{2,1,0:T(8,128)(2,1)}, u32[]{:S(2)}) copy-start(bf16[2,512,512]{2,1,0:T(8,128)(2,1)} %param.24) | copy-start | bytes 3145732
  453.3 21.5 %copy-start.7 = (bf16[2,512,512]{2,1,0:T(8,128)(2,1)S(1)}, bf16[2,512,512]{2,1,0:T(8,128)(2,1)}, u32[]{:S(2)}) copy-start(bf16[2,512,512]{2,1,0:T(8,128)(2,1)} %param.25) | copy-start | bytes 3145732
  495.9 2.2 copy-start.6
where the time goes:
time: 557 us; the launch traced here: 548 us
  blocking collectives  286 us (51%)
  local copies, waits for them, and re-layouts  170 us (31%)
  matrix products  73.6 us (13%)
  other arithmetic  11 us (2%)
    unnamed x1, blocking collectives  234 us
    reshape x16, local copies, waits for them, and re-layouts, pick_rows(): flat_rows = cache_blk.reshape(n_layers, local_beams, -1)  122 us
    dot_general x8, matrix products, pick_rows(): jnp.einsum('rc,lcx->lrx', one_hot, flat_rows, preferred_element_type=jnp....  39 us
    psum x2, blocking collectives, local_step(): mix_sum, exp_total = lax.psum((part_mix, part_sum), 'sp')  29.6 us
    pmax x2, blocking collectives, local_step(): row_max = lax.pmax(jnp.max(scores, axis=-1, keepdims=True), 'sp')  22 us
    unnamed x25, local copies, waits for them, and re-layouts  17.8 us
    dot_general x1, matrix products, local_step(): logits = jnp.dot(hidden, w_vocab, preferred_element_type=jnp.float32)  12.8 us
  transfers between devices with their start and end apart: 6, of which 0 were waited for; matrix products, arithmetic and copies ran while one was open for 29% of the time, Pallas kernels for 0%

commit v1 on v0

v1 whole, which is shorter than its diff:
```python
import functools

import jax
import jax.numpy as jnp
from jax import lax
from jax.experimental import pallas as pl
from jax.experimental.pallas import tpu as pltpu
from jax.sharding import PartitionSpec as P

ROPE_BASE = 10000.0
NORM_EPS = 1e-6
NEG = -1e30
CORES = 2
LEVELS = (12,)
CHUNK = 2048
VBUF = 4
VMEM_LIMIT = 64 * 1024 * 1024 - 64 * 1024
MESH = pl.DeviceIdType.MESH
F32 = jnp.float32
BF16 = jnp.bfloat16


def rms(x, g):
    ms = jnp.mean(x * x, axis=-1, keepdims=True)
    return (x * lax.rsqrt(ms + NORM_EPS) * g.astype(F32)).astype(BF16)


def plan_kernel(dims, parent_ref, score_ref, tok_ref, plan_ref, pay_ref, pm_ref, rank_ref):
    nb, span = dims
    rows = CORES * nb
    n_sent, width = parent_ref.shape
    me = lax.axis_index('beam')
    sent = me // span
    place = lax.rem(me, span)
    chip = lax.div(place, CORES)

    def needed(s, to_chip):
        base = (1 - to_chip) * rows
        mask = jnp.int32(0)
        for k in range(rows):
            p = parent_ref[s, to_chip * rows + k] - s * width - base
            mask = mask | jnp.where((p >= 0) & (p < rows), jnp.left_shift(jnp.int32(1), jnp.clip(p, 0, rows - 1)), 0)
        return mask

    def bit(mask, p):
        return jnp.right_shift(mask, p) & 1

    most = jnp.int32(0)
    for s in range(n_sent):
        for tc in range(2):
            m = needed(s, tc)
            most = jnp.maximum(most, sum(bit(m, p) for p in range(rows)))
    out_mask = needed(sent, 1 - chip)
    in_mask = needed(sent, chip)
    for p in range(rows + 1):
        plan_ref[p] = 0
    cnt = jnp.int32(0)
    for p in range(rows):
        @pl.when(bit(out_mask, p) == 1)
        def _(p=p, cnt=cnt):
            plan_ref[cnt] = p
        cnt = cnt + bit(out_mask, p)
    cnt = jnp.int32(0)
    for p in range(rows):
        rank_ref[p] = cnt
        cnt = cnt + bit(in_mask, p)
    for b in range(nb):
        par = parent_ref[sent, place * nb + b] - sent * width
        dev = lax.div(par, nb)
        row = lax.rem(par, nb)
        far = lax.div(dev, CORES) != chip
        slot = rank_ref[jnp.clip(par - (1 - chip) * rows, 0, rows - 1)]
        plan_ref[rows + b] = jnp.where(far, 2, jnp.where(dev == place, 0, 1))
        plan_ref[rows + nb + b] = jnp.where(far, slot, row)
    plan_ref[rows + 2 * nb] = most
    for i in range(span):
        for b in range(8):
            if b < nb:
                par = parent_ref[sent, i * nb + b] - sent * width
                code = lax.div(par, nb) * 8 + lax.rem(par, nb)
            else:
                code = jnp.int32(-1)
            pm_ref[i * 8 + b:i * 8 + b + 1, :] = jnp.full((1, pm_ref.shape[1]), code, jnp.int32)
    lane = lax.broadcasted_iota(jnp.int32, (1, pay_ref.shape[1]), 1)
    row = jnp.zeros((1, pay_ref.shape[1]), F32)
    for b in range(nb):
        row = jnp.where(lane == b, score_ref[b], row)
    pay_ref[0:nb, :] = tok_ref[...].astype(F32)
    pay_ref[nb:nb + 1, :] = row
    pay_ref[nb + 1:8, :] = jnp.zeros((8 - nb - 1, pay_ref.shape[1]), F32)


def main_kernel(dims, n_slots, plan_ref, pos_ref, pay_ref, pm_ref, cs_ref, ga_ref, gm_ref, gf_ref,
                k_ref, v_ref, wq_ref, wk_ref, wv_ref, wo_ref, wg_ref, wu_ref, wd_ref, wvoc_ref,
                cand_ref, new_ref, sib_ref, recv_ref,
                pk0, pk1, pk2, pk3, stage, kv_att, b_q, b_k, b_v, b_o, b_g, b_u, b_d, vbuf,
                payall, resid, qbuf, knew, vnew, pbuf, rbuf, abuf, gbuf, attn,
                s_pl, s_pr, s_pkl, s_pks, s_pkr, s_sib, s_ss, s_sr, s_bs, s_br, s_fs, s_fr,
                s_att, s_w, s_voc, s_1s, s_1r, s_2s, s_2r):
    nb, span, sp_n, hd = dims
    n_layers = ga_ref.shape[0]
    dm = ga_ref.shape[1]
    slots = k_ref.shape[3]
    half = k_ref.shape[2] // 2
    seq = lax.axis_index('sp')
    me = lax.axis_index('beam')
    place = lax.rem(me, span)
    base = me - place
    core = lax.rem(me, CORES)
    other = 1 - core
    rows = CORES * nb
    sib = {'beam': base + lax.div(place, CORES) * CORES + other}
    par = {'beam': base + lax.rem(place + CORES, span)}

    def peer(di, dj):
        return {'beam': base + lax.rem(place + di, span), 'sp': lax.rem(seq + dj, sp_n)}

    everyone = [(di, dj) for di in range(span) for dj in range(sp_n) if (di, dj) != (0, 0)]

    barrier = pltpu.get_barrier_semaphore()
    for di, dj in everyone:
        pl.semaphore_signal(barrier, inc=1, device_id=peer(di, dj), device_id_type=MESH)

    def local(src, dst, sem):
        c = pltpu.make_async_copy(src, dst, sem)
        c.start()
        return c

    def remote(src, dst, ss, rs, dev):
        return pltpu.make_async_remote_copy(src_ref=src, dst_ref=dst, send_sem=ss, recv_sem=rs,
                                            device_id=dev, device_id_type=MESH)

    pks = (pk0, pk1, pk2, pk3)
    chunks = [(src, pl.ds(h * half, half)) for src in (k_ref, v_ref) for h in range(2)]
    pk_local = [local(src.at[core, :, hs], pks[i].at[pl.ds(core * nb, nb)], s_pkl.at[i])
                for i, (src, hs) in enumerate(chunks)]
    w0 = [local(src.at[0], dst.at[0], s_w.at[0, i])
          for i, (src, dst) in enumerate(((wq_ref, b_q), (wk_ref, b_k), (wv_ref, b_v)))]
    att = {}
    for l in range(n_layers):
        for i, src in enumerate((k_ref, v_ref)):
            att[l, i] = local(src.at[l], kv_att.at[l, i], s_att.at[l, i])
    weights = {}
    pairs = ((wq_ref, b_q), (wk_ref, b_k), (wv_ref, b_v), (wo_ref, b_o), (wg_ref, b_g), (wu_ref, b_u), (wd_ref, b_d))
    for l in range(n_layers):
        for i, (src, dst) in enumerate(pairs):
            weights[l, i] = w0[i] if (l == 0 and i < 3) else local(src.at[l], dst.at[l], s_w.at[l, i])
    vocab = wvoc_ref.shape[1]
    n_full = vocab // CHUNK
    tail = vocab - n_full * CHUNK

    def voc_copy(i, slot):
        return pltpu.make_async_copy(wvoc_ref.at[:, pl.ds(i * CHUNK, CHUNK)], vbuf.at[slot], s_voc.at[slot])

    def voc_tail():
        return pltpu.make_async_copy(wvoc_ref.at[:, pl.ds(n_full * CHUNK, tail)],
                                     vbuf.at[n_full % VBUF, :, pl.ds(0, tail)], s_voc.at[n_full % VBUF])

    for i in range(VBUF):
        voc_copy(i, i).start()

    pl.semaphore_wait(barrier, len(everyone))

    pay_out = []
    for di in range(1, span):
        c = remote(pay_ref, payall.at[di], s_pl.at[di], s_pr.at[di], peer(di, 0))
        c.start()
        pay_out.append(c)
    sib_pk = []
    for i, (src, hs) in enumerate(chunks):
        c = remote(src.at[other, :, hs], pks[i].at[pl.ds(core * nb, nb)], s_pks.at[i], s_pkr.at[i], sib)
        c.start()
        sib_pk.append(c)
    sib_rest = []
    for i, src in enumerate((k_ref, v_ref)):
        c = remote(src.at[core], sib_ref.at[core, i], s_ss.at[i], s_sr.at[i], sib)
        c.start()
        sib_rest.append(c)

    def bulk(ch, s):
        dst = recv_ref.at[core, ch // 2, s, pl.ds((ch % 2) * half, half)]
        return remote(stage.at[ch, s], dst, s_bs.at[ch, s], s_br.at[ch, s], par)

    def forward(ch, s):
        ref = recv_ref.at[core, ch // 2, s, pl.ds((ch % 2) * half, half)]
        return remote(ref, ref, s_fs.at[ch, s], s_fr.at[ch, s], sib)

    sib_home = []

    def pack(ch):
        pk_local[ch].wait()
        sib_pk[ch].wait_recv()
        for s in range(n_slots):
            stage[ch, s] = pks[ch][plan_ref[s]]
        hs = pl.ds((ch % 2) * half, half)
        sib_home.append(local(pks[ch].at[pl.ds(other * nb, nb)], sib_ref.at[core, ch // 2, :, hs], s_sib.at[ch]))

    units = [(ch, s) for ch in range(4) for s in range(n_slots)]
    issued = [0]

    def issue(count):
        for ch, s in units[issued[0]:issued[0] + count]:
            bulk(ch, s).start()
        issued[0] = min(len(units), issued[0] + count)

    pack(0)
    issue(min(3, n_slots))

    payall[0] = pay_ref[...]
    for c in pay_out:
        c.wait_recv()
    for i in range(span):
        resid[pl.ds(pl.multiple_of(i * 8, 8), 8), :] = payall[lax.rem(place - i + span, span)]

    lane = lax.broadcasted_iota(jnp.int32, (1, dm), 1)
    low = lax.rem(lane, hd) < hd // 2
    t = pos_ref[0]
    att_scale = hd ** -0.5
    cosv = cs_ref[0:1, :]
    sinv = cs_ref[1:2, :]

    def rope(x):
        swapped = jnp.where(low, pltpu.roll(x, dm - hd // 2, 1), pltpu.roll(x, hd // 2, 1))
        return x * cosv + swapped * sinv

    qw = 256
    hq = qw // hd
    n_quad = dm // qw
    lane_q = lax.broadcasted_iota(jnp.int32, (1, qw), 1)
    head_mask = [lax.div(lane_q, hd) == h for h in range(hq)]
    slot_id = seq * slots + lax.broadcasted_iota(jnp.int32, (1, slots), 1)
    valid = slot_id < t
    pm = pm_ref[...]
    pm4 = jnp.concatenate([pm] * hq, axis=0)
    nrow = pm.shape[0]

    for l in range(n_layers):
        hidden = rms(resid[...], ga_ref[l:l + 1, :])
        for i in range(3):
            weights[l, i].wait()
        q = jnp.dot(hidden, b_q[l], preferred_element_type=F32).astype(BF16).astype(F32)
        k = jnp.dot(hidden, b_k[l], preferred_element_type=F32).astype(BF16).astype(F32)
        v = jnp.dot(hidden, b_v[l], preferred_element_type=F32).astype(BF16).astype(F32)
        q = rope(q).astype(BF16).astype(F32)
        k = rope(k).astype(BF16).astype(F32)
        qbuf[...] = q
        knew[...] = k
        vnew[...] = v
        mine = pl.ds(pl.multiple_of(place * 8, 8), 8)
        new_ref[l, 0] = knew[mine, :]
        new_ref[l, 1] = vnew[mine, :]
        if l == 0:
            for ch in range(1, 4):
                pack(ch)
        att[l, 0].wait()
        att[l, 1].wait()
        for g in range(n_quad):
            gs = pl.ds(g * qw, qw)
            qg = q[:, g * qw:(g + 1) * qw]
            qq = jnp.concatenate([jnp.where(hm, qg, 0.0) for hm in head_mask], axis=0).astype(BF16)
            s = jnp.zeros((hq * nrow, slots), F32)
            for c in range(nb):
                sc = jnp.dot(qq, kv_att[l, 0, c, gs], preferred_element_type=F32)
                s = jnp.where(pm4 == place * 8 + c, sc, s)
            s = jnp.where(valid, s * att_scale, NEG)
            m = jnp.max(s, axis=-1, keepdims=True)
            e = jnp.where(valid, jnp.exp(s - m), 0.0)
            den = jnp.sum(e, axis=-1, keepdims=True)
            acc = jnp.zeros((hq * nrow, qw), F32)
            for c in range(nb):
                ec = jnp.where(pm4 == place * 8 + c, e, 0.0).astype(BF16)
                acc = acc + lax.dot_general(ec, kv_att[l, 1, c, gs], (((1,), (1,)), ((), ())),
                                            preferred_element_type=F32)

            def fold(x):
                y = jnp.zeros((nrow, qw), F32)
                for h in range(hq):
                    y = jnp.where(head_mask[h], x[h * nrow:(h + 1) * nrow], y)
                return y

            for j, x in enumerate((fold(acc), fold(m), fold(den))):
                for w in range(qw // 128):
                    pbuf[l, g * (qw // 128) + w, j] = x[:, w * 128:(w + 1) * 128]
        ex1 = []
        for dj in range(1, sp_n):
            c = remote(pbuf.at[l, lax.rem(seq + dj, sp_n)], rbuf.at[l, dj], s_1s.at[l, dj], s_1r.at[l, dj], peer(0, dj))
            c.start()
            ex1.append(c)
        rbuf[l, 0] = pbuf[l, seq]
        js = pl.ds(pl.multiple_of(seq * 128, 128), 128)
        prod = qbuf[:, js] * knew[:, js]
        lane2 = lax.broadcasted_iota(jnp.int32, (1, 128), 1)
        s_new = jnp.zeros((nrow, 128), F32)
        for h in range(128 // hd):
            hm = lax.div(lane2, hd) == h
            s_new = jnp.where(hm, jnp.sum(jnp.where(hm, prod, 0.0), axis=-1, keepdims=True), s_new)
        s_new = s_new * att_scale
        for c in ex1:
            c.wait_recv()
        m_all = s_new
        for dj in range(sp_n):
            m_all = jnp.maximum(m_all, rbuf[l, dj, 1])
        w_new = jnp.exp(s_new - m_all)
        num = w_new * vnew[:, js]
        den = w_new
        for dj in range(sp_n):
            wj = jnp.exp(rbuf[l, dj, 1] - m_all)
            num = num + wj * rbuf[l, dj, 0]
            den = den + wj * rbuf[l, dj, 2]
        o = jnp.where(lax.div(pm[:, 0:128], 8) == place, num / den, 0.0).astype(BF16)
        abuf[l] = o
        ex2 = []
        for n, (di, dj) in enumerate(everyone):
            c = remote(abuf.at[l], gbuf.at[l, n + 1], s_2s.at[l, n], s_2r.at[l, n], peer(di, dj))
            c.start()
            ex2.append(c)
        issue(4 if l == 0 else len(units))
        gbuf[l, 0] = o
        for i in range(3, 7):
            weights[l, i].wait()
        for c in ex2:
            c.wait_recv()
        for dj in range(sp_n):
            total = gbuf[l, dj].astype(F32)
            for di in range(1, span):
                total = total + gbuf[l, di * sp_n + dj].astype(F32)
            off = pl.multiple_of(lax.rem(seq - dj + sp_n, sp_n) * 128, 128)
            attn[:, pl.ds(off, 128)] = total
        r = resid[...]
        r = r + jnp.dot(attn[...].astype(BF16), b_o[l], preferred_element_type=F32).astype(BF16).astype(F32)
        hidden = rms(r, gm_ref[l:l + 1, :])
        gate = jnp.dot(hidden, b_g[l], preferred_element_type=F32).astype(BF16).astype(F32)
        up = jnp.dot(hidden, b_u[l], preferred_element_type=F32).astype(BF16).astype(F32)
        act = (gate * jax.nn.sigmoid(gate) * up).astype(BF16)
        r = r + jnp.dot(act, b_d[l], preferred_element_type=F32).astype(BF16).astype(F32)
        resid[...] = r
        for c in ex1 + ex2:
            c.wait_send()

    own = resid[pl.ds(pl.multiple_of(place * 8, 8), 8), :]
    hv = rms(own, gf_ref[...])

    @pl.loop(0, n_full)
    def _(i):
        slot = lax.rem(i, VBUF)
        voc_copy(i, slot).wait()
        cand_ref[:, pl.ds(pl.multiple_of(i * CHUNK, CHUNK), CHUNK)] = jnp.dot(
            hv, vbuf[slot], preferred_element_type=F32)

        @pl.when(i + VBUF < n_full)
        def _():
            voc_copy(i + VBUF, slot).start()

        if tail:
            @pl.when(i + VBUF == n_full)
            def _():
                voc_tail().start()

    if tail:
        voc_tail().wait()
        cand_ref[:, pl.ds(n_full * CHUNK, tail)] = jnp.dot(
            hv, vbuf[n_full % VBUF, :, pl.ds(0, tail)], preferred_element_type=F32)

    lg = cand_ref[...]
    mx = jnp.max(lg, axis=-1, keepdims=True)
    lse = jnp.log(jnp.sum(jnp.exp(lg - mx), axis=-1, keepdims=True))
    code = pm_ref[pl.ds(pl.multiple_of(place * 8, 8), 8), 0:128]
    lane1 = lax.broadcasted_iota(jnp.int32, (1, 128), 1)
    score = jnp.zeros((8, 1), F32)
    for i in range(span):
        dev = lax.rem(place - i + span, span)
        srow = payall[i, nb:nb + 1, 0:128]
        score = score + jnp.sum(jnp.where(code == dev * 8 + lane1, srow, 0.0), axis=-1, keepdims=True)
    cand_ref[...] = score + ((cand_ref[...] - mx) - lse)

    for ch in range(4):
        @pl.loop(0, n_slots)
        def _(s, ch=ch):
            bulk(ch, s).wait_recv()
            forward(ch, s).start()
    for c in pay_out + sib_pk + sib_rest:
        c.wait_send()
    for c in sib_rest:
        c.wait_recv()
    for c in sib_home:
        c.wait()
    for ch in range(4):
        @pl.loop(0, n_slots)
        def _(s, ch=ch):
            bulk(ch, s).wait_send()
            forward(ch, s).wait_send()
            ref = recv_ref.at[other, ch // 2, s, pl.ds((ch % 2) * half, half)]
            remote(ref, ref, s_fs.at[ch, s], s_fr.at[ch, s], sib).wait_recv()


def assemble_kernel(dims, plan_ref, pos_ref, new_ref, cand8_ref, k_ref, v_ref, sib_ref, recv_ref,
                    ko_ref, vo_ref, cand_ref, buf, s_in, s_out):
    nb = dims[0]
    rows = CORES * nb
    n_layers = k_ref.shape[0]
    slots = k_ref.shape[3]
    seq = lax.axis_index('sp')
    at = pos_ref[0] - seq * slots
    owns = (at >= 0) & (at < slots)
    order = [(l, i, b) for l in range(n_layers) for i in range(2) for b in range(nb)]
    for u, (l, i, b) in enumerate(order):
        kind = plan_ref[rows + b]
        idx = plan_ref[rows + nb + b]
        src = (k_ref, v_ref)[i]

        @pl.when(kind == 0)
        def _():
            pltpu.make_async_copy(src.at[l, idx], buf.at[u], s_in.at[u]).start()

        @pl.when(kind == 1)
        def _():
            pltpu.make_async_copy(sib_ref.at[l, i, idx], buf.at[u], s_in.at[u]).start()

        @pl.when(kind == 2)
        def _():
            pltpu.make_async_copy(recv_ref.at[l, i, idx], buf.at[u], s_in.at[u]).start()

    cand_ref[...] = cand8_ref[0:nb, :]
    tile = jnp.clip(lax.div(at, 128), 0, slots // 128 - 1)
    lane = lax.broadcasted_iota(jnp.int32, (1, 128), 1)
    outs = []
    for l in range(n_layers):
        for i in range(2):
            cols = jnp.transpose(new_ref[l, i])
            for b in range(nb):
                u = (l * 2 + i) * nb + b
                pltpu.make_async_copy((k_ref, v_ref)[i].at[l, b], buf.at[u], s_in.at[u]).wait()

                @pl.when(owns)
                def _():
                    ts = pl.ds(pl.multiple_of(tile * 128, 128), 128)
                    old = buf[u, :, ts]
                    buf[u, :, ts] = jnp.where(lane == at - tile * 128, cols[:, b:b + 1].astype(BF16), old)

                c = pltpu.make_async_copy(buf.at[u], (ko_ref, vo_ref)[i].at[l, b], s_out.at[u])
                c.start()
                outs.append(c)
    for c in outs:
        c.wait()


def solution(mesh):
    beam_spec = P(('dp', 'beam'))
    row_spec = P(('dp', 'beam'), None)
    cache_spec = P(None, ('dp', 'beam'), 'sp', None, None)
    rep = P()
    sp_n = mesh.shape['sp']

    def local_step(tok_emb, parent, position, beam_score, k_cache, v_cache, w_query, w_key, w_value, w_out,
                   w_gate, w_up, w_down, g_attn, g_mlp, g_final, w_vocab):
        n_layers, nb, slots, heads, hd = k_cache.shape
        width = parent.shape[1]
        span = width // nb
        dm = tok_emb.shape[1]
        ff = w_gate.shape[2]
        vocab = w_vocab.shape[1]
        rows = CORES * nb
        hrow = heads * hd
        kt = k_cache.transpose(0, 1, 3, 4, 2).reshape(n_layers, nb, hrow, slots)
        vt = v_cache.transpose(0, 1, 3, 4, 2).reshape(n_layers, nb, hrow, slots)
        smem = pl.BlockSpec(memory_space=pltpu.SMEM)
        vmem = pl.BlockSpec(memory_space=pltpu.VMEM)
        hbm = pl.BlockSpec(memory_space=pl.ANY)
        sds = jax.ShapeDtypeStruct

        plan, pay, pm = pl.pallas_call(
            functools.partial(plan_kernel, (nb, span)),
            out_shape=(sds((64,), jnp.int32), sds((8, dm), F32), sds((8 * span, slots), jnp.int32)),
            in_specs=[smem, smem, vmem], out_specs=(smem, vmem, vmem),
            scratch_shapes=[pltpu.SMEM((rows,), jnp.int32)],
            name='plan',
        )(parent, beam_score, tok_emb)

        half_dim = hd // 2
        inv_freq = ROPE_BASE ** (-2.0 * jnp.arange(half_dim, dtype=F32) / hd)
        angles = position[0].astype(F32) * inv_freq
        cos_t, sin_t = jnp.cos(angles), jnp.sin(angles)
        cs = jnp.stack([jnp.tile(jnp.concatenate([cos_t, cos_t]), heads),
                        jnp.tile(jnp.concatenate([-sin_t, sin_t]), heads)])

        def main(n_slots, cid, *ops):
            half = hrow // 2
            np_ = dm // 128
            nrow = 8 * span
            dma = pltpu.SemaphoreType.DMA
            scratch = [pltpu.VMEM((rows, half, slots), BF16)] * 4 + [
                pltpu.VMEM((4, n_slots, half, slots), BF16),
                pltpu.VMEM((n_layers, 2, nb, hrow, slots), BF16),
                pltpu.VMEM((n_layers, dm, hrow), BF16),
                pltpu.VMEM((n_layers, dm, hrow), BF16),
                pltpu.VMEM((n_layers, dm, hrow), BF16),
                pltpu.VMEM((n_layers, hrow, dm), BF16),
                pltpu.VMEM((n_layers, dm, ff), BF16),
                pltpu.VMEM((n_layers, dm, ff), BF16),
                pltpu.VMEM((n_layers, ff, dm), BF16),
                pltpu.VMEM((VBUF, dm, CHUNK), BF16),
                pltpu.VMEM((span, 8, dm), F32),
                pltpu.VMEM((nrow, dm), F32),
                pltpu.VMEM((nrow, dm), F32),
                pltpu.VMEM((nrow, dm), F32),
                pltpu.VMEM((nrow, dm), F32),
                pltpu.VMEM((n_layers, np_, 3, nrow, 128), F32),
                pltpu.VMEM((n_layers, sp_n, 3, nrow, 128), F32),
                pltpu.VMEM((n_layers, nrow, 128), BF16),
                pltpu.VMEM((n_layers, span * sp_n, nrow, 128), BF16),
                pltpu.VMEM((nrow, dm), F32),
                dma((span,)), dma((span,)),
                dma((4,)), dma((4,)), dma((4,)), dma((4,)), dma((2,)), dma((2,)),
                dma((4, n_slots)), dma((4, n_slots)), dma((4, n_slots)), dma((4, n_slots)),
                dma((n_layers, 2)), dma((n_layers, 7)), dma((VBUF,)),
                dma((n_layers, sp_n)), dma((n_layers, sp_n)),
                dma((n_layers, span * sp_n)), dma((n_layers, span * sp_n)),
            ]
            return pl.pallas_call(
                functools.partial(main_kernel, (nb, span, sp_n, hd), n_slots),
                out_shape=(sds((8, vocab), F32), sds((n_layers, 2, 8, hrow), F32),
                           sds((n_layers, 2, nb, hrow, slots), BF16),
                           sds((n_layers, 2, rows, hrow, slots), BF16)),
                in_specs=[smem, smem] + [vmem] * 6 + [hbm] * 10,
                out_specs=(vmem, vmem, hbm, hbm),
                scratch_shapes=scratch,
                compiler_params=pltpu.CompilerParams(collective_id=cid, has_side_effects=True,
                                                     vmem_limit_bytes=VMEM_LIMIT),
                name=f'main{n_slots}',
            )(*ops)

        ops = (plan, position, pay, pm, cs, g_attn, g_mlp, g_final.reshape(1, dm), kt, vt,
               w_query, w_key, w_value, w_out, w_gate, w_up, w_down, w_vocab)
        cand8, new, sib, recv = main(LEVELS[-1], 0, *ops)

        ko, vo, cand = pl.pallas_call(
            functools.partial(assemble_kernel, (nb,)),
            out_shape=(sds(kt.shape, BF16), sds(vt.shape, BF16), sds((nb, vocab), F32)),
            in_specs=[smem, smem, vmem, vmem, hbm, hbm, hbm, hbm],
            out_specs=(hbm, hbm, vmem),
            scratch_shapes=[pltpu.VMEM((n_layers * 2 * nb, hrow, slots), BF16),
                            pltpu.SemaphoreType.DMA((n_layers * 2 * nb,)),
                            pltpu.SemaphoreType.DMA((n_layers * 2 * nb,))],
            compiler_params=pltpu.CompilerParams(vmem_limit_bytes=VMEM_LIMIT),
            name='assemble',
        )(plan, position, new, cand8, kt, vt, sib, recv)

        def back(x):
            return x.reshape(n_layers, nb, heads, hd, slots).transpose(0, 1, 4, 2, 3)

        return back(ko), back(vo), cand

    in_specs = (row_spec, P('dp', None), rep, beam_spec, cache_spec, cache_spec) + (rep,) * 11
    return jax.shard_map(local_step, mesh=mesh, in_specs=in_specs, out_specs=(cache_spec, cache_spec, row_spec),
                         check_vma=False)
```

time: 557 us -> 171 us (0.31)
  the two profiles are of different devices: /device:TPU:96 before, /device:TPU:97 now
where the time goes in v1:
time: 171 us
  Pallas kernels  168 us (98%)
    pallas_call x1, Pallas kernels, main(): pl.pallas_call(functools.partial(main_kernel, (nb, span, sp_n, hd), n_slo...  157 us
    pallas_call x1, Pallas kernels, local_step(): pl.pallas_call(functools.partial(assemble_kernel, (nb,)), out_shape=(sds(...  8.43 us

profile of v1, /device:TPU:97, one launch (start us, length us, event | category | flops | bytes accessed | tf_op | source)
XLA Modules:
  0.0 171.2 jit_solution(7824235662368002417)
XLA Ops:
  1.3 0.1 fusion.2
  1.3 0.1 fusion
  1.4 0.1 pad_maximum_fusion.2
  1.5 0.1 pad_maximum_fusion.1
  1.5 1.3 reshape.24.gf_ref
  2.8 0.1 stack_tile.6
  2.9 0.1 stack_tile.7
  3.0 0.6 pad_maximum_fusion.cs_ref
  3.6 1.9 %plan.1 = (s32[64]{0:T(128)}, f32[8,512]{1,0:T(8,128)}, s32[32,256]{1,0:T(8,128)}) custom-call(s32[2,24]{1,0:T(2,128)} %parent_ref.1, f32[6]{0:T(128)} %score_ref.1, bf16[6,512]{1,0:T(8,128)(2,1)} %tok_ref.1), custom_call_target="tpu_custom_call" | custom-call | tf_op jit(solution)/shard_map/plan/pallas_call | solution.py:471
  5.5 157.3 %main12.1 = (f32[8,32128]{1,0:T(8,128)}, f32[2,2,8,512]{3,2,1,0:T(8,128)}, bf16[2,2,6,512,256]{4,3,2,1,0:T(8,128)(2,1)}, bf16[2,2,12,512,256]{4,3,2,1,0:T(8,128)(2,1)}) custom-call(s32[64]{0:T(128)} %get-tuple-element.13.plan_ref, s32[1]{0:T(128)S(6)} %copy.20.pos_ref, f32[8,512]{1,0:T(8,128)} %get-tuple-element.14.pay_ref, ...), custom_call_target="tpu_custom_call" | custom-call | tf_op jit(solution)/shard_map/main12/pallas_call | solution.py:519
  162.8 8.4 %assemble.1 = (bf16[2,6,512,256]{3,2,1,0:T(8,128)(2,1)}, bf16[2,6,512,256]{3,2,1,0:T(8,128)(2,1)}, f32[6,32128]{1,0:T(8,128)}) custom-call(s32[64]{0:T(128)} %get-tuple-element.13.plan_ref, s32[1]{0:T(128)S(6)} %copy.20.pos_ref, f32[2,2,8,512]{3,2,1,0:T(8,128)} %get-tuple-element.16.new_ref, f32[8,32128]{1,0:T(8,128)} %get-tuple-element.17.cand8_ref, ...), custom_call_target="tpu_custom_call" | custom-call | tf_op jit(solution)/shard_map/assemble/pallas_call | solution.py:536
  (2 shorter events, 0.0 us)

commit v2 on v1

--- a/solution.py
+++ b/solution.py
@@ -11,7 +11,7 @@
 NORM_EPS = 1e-6
 NEG = -1e30
 CORES = 2
-LEVELS = (12,)
+LEVELS = (3, 4, 5, 6)
 CHUNK = 2048
 VBUF = 4
 VMEM_LIMIT = 64 * 1024 * 1024 - 64 * 1024
@@ -531,7 +531,11 @@
 
         ops = (plan, position, pay, pm, cs, g_attn, g_mlp, g_final.reshape(1, dm), kt, vt,
                w_query, w_key, w_value, w_out, w_gate, w_up, w_down, w_vocab)
-        cand8, new, sib, recv = main(LEVELS[-1], 0, *ops)
+        levels = [n for n in LEVELS if n < rows] + [rows]
+        most = plan[rows + 2 * nb]
+        branch = sum((most > n).astype(jnp.int32) for n in levels[:-1])
+        cand8, new, sib, recv = lax.switch(
+            branch, [functools.partial(main, n, i) for i, n in enumerate(levels)], *ops)
 
         ko, vo, cand = pl.pallas_call(
             functools.partial(assemble_kernel, (nb,)),

time: 171 us -> 85.4 us (0.50)
  Pallas kernels: 168 us -> 76.9 us
  between operations: 1.31 us -> 4.04 us
    pallas_call x1, Pallas kernels: 157 us -> 66.8 us  [main(): pl.pallas_call(functools.partial(main_kernel, (nb, span, sp_n, hd), n_slo...]
where the time goes in v2:
time: 85.4 us; the launch traced here: 85.2 us
  Pallas kernels  76.9 us (90%)
  between operations  4.04 us (5%)
  local copies, waits for them, and re-layouts  2.71 us (3%)
  other arithmetic  0.86 us (1%)
    pallas_call x1, Pallas kernels, main(): pl.pallas_call(functools.partial(main_kernel, (nb, span, sp_n, hd), n_slo...  66.8 us
    pallas_call x1, Pallas kernels, local_step(): pl.pallas_call(functools.partial(assemble_kernel, (nb,)), out_shape=(sds(...  8.16 us
    pallas_call x1, Pallas kernels, local_step(): pl.pallas_call(functools.partial(plan_kernel, (nb, span)), out_shape=(sds...  1.86 us

profile of v2, /device:TPU:97, one launch (start us, length us, event | category | flops | bytes accessed | tf_op | source)
XLA Modules:
  0.0 85.2 jit_solution(9709978546532132498)
XLA Ops:
  1.3 0.1 fusion.2
  1.3 0.1 fusion
  1.4 0.1 pad_maximum_fusion.2
  1.5 0.1 pad_maximum_fusion.1
  1.5 1.3 %reshape.39 = bf16[1,512]{1,0:T(2,128)(2,1)} reshape(bf16[512]{0:T(512)(128)(2,1)} %param.37) | data formatting | bytes 2048 | tf_op jit(solution)/shard_map/reshape | solution.py:532
  2.8 0.1 stack_tile.6
  2.9 0.1 stack_tile.7
  3.0 0.6 pad_maximum_fusion
  3.6 1.9 %plan.1 = (s32[64]{0:T(128)}, f32[8,512]{1,0:T(8,128)}, s32[32,256]{1,0:T(8,128)}) custom-call(s32[2,24]{1,0:T(2,128)} %parent_ref.1, f32[6]{0:T(128)} %score_ref.1, bf16[6,512]{1,0:T(8,128)(2,1)} %tok_ref.1), custom_call_target="tpu_custom_call" | custom-call | tf_op jit(solution)/shard_map/plan/pallas_call | solution.py:471
  5.4 1.3 %slice.3 = s32[1]{0:T(128)} slice(s32[64]{0:T(128)} %get-tuple-element.283.plan_ref), slice={[24:25]} | slice | bytes 8 | tf_op jit(solution)/shard_map/slice | solution.py:535
  9.2 67.6 %conditional.1 = ((f32[8,32128]{1,0:T(8,128)}, f32[2,2,8,512]{3,2,1,0:T(8,128)}, bf16[2,2,6,512,256]{4,3,2,1,0:T(8,128)(2,1)}, bf16[2,2,12,512,256]{4,3,2,1,0:T(8,128)(2,1)})) conditional(s32[]{:T(128)} %bitcast, (s32[64]{0:T(128)}, s32[1]{0:T(128)}, f32[8,512]{1,0:T(8,128)}, s32[32,256]{1,0:T(8,128)}, ...), branch_computations={%region_0.0_spmd, %region_1.0_spmd, %region_2.0_spmd, %region_3.0_... | conditional | bytes 8 | solution.py:537
  9.4 66.8 %main4.1 = (f32[8,32128]{1,0:T(8,128)}, f32[2,2,8,512]{3,2,1,0:T(8,128)}, bf16[2,2,6,512,256]{4,3,2,1,0:T(8,128)(2,1)}, bf16[2,2,12,512,256]{4,3,2,1,0:T(8,128)(2,1)}) custom-call(s32[64]{0:T(128)} %get-tuple-element.198.plan_ref, s32[1]{0:T(128)} %get-tuple-element.199.pos_ref, f32[8,512]{1,0:T(8,128)} %get-tuple-element.200.pay_ref, ...), custom_call_target="tpu_custom_call" | custom-call | tf_op jit(solution)/shard_map/cond/branch_1_fun/main4/pallas_call | solution.py:519
  76.8 8.2 %assemble.1 = (bf16[2,6,512,256]{3,2,1,0:T(8,128)(2,1)}, bf16[2,6,512,256]{3,2,1,0:T(8,128)(2,1)}, f32[6,32128]{1,0:T(8,128)}) custom-call(s32[64]{0:T(128)} %get-tuple-element.283.plan_ref, s32[1]{0:T(128)S(6)} %copy.40.pos_ref, f32[2,2,8,512]{3,2,1,0:T(8,128)} %get-tuple-element.286.new_ref, f32[8,32128]{1,0:T(8,128)} %get-tuple-element.287.cand8_ref, ...), custom_call_target="tpu_custom_call" | custom-call | tf_op jit(solution)/shard_map/assemble/pallas_call | solution.py:540
  (2 shorter events, 0.0 us)
